TPU v7x, 32 devices: a whole 2x2x4 slice. The times are simulated.
32 devices in a mesh: gx: 4 (over y, x), gy: 2 (over core), gz: 4 (over z).
Axes of the slice: x: 2, y: 2, z: 4, core: 2. Of those that a mesh axis runs over, the one named last changes fastest.
Arguments:
- gradient: bfloat16 [32, 32, 16, 512], P(None, 'gx', 'gy', 'gz'), may hold values from -6 to 6
- noise_draw: bfloat16 [32, 32, 16, 512], P(None, 'gx', 'gy', 'gz'), may hold values from -6 to 6
- current: float32 [32, 32, 16, 512], P(None, 'gx', 'gy', 'gz'), may hold values from -6 to 6
- eigvectors: bfloat16 [32, 16, 512, 512], P('gx', 'gy', 'gz'), may hold values from -0.125 to 0.125
- eigvalues: float32 [512], replicated, may hold values from 0.05 to 50
- reaction: float32 [32, 16, 512], P('gx', 'gy', 'gz'), may hold values from 0.25 to 4
Outputs:
- proposal: float32 [32, 32, 16, 512], P(None, 'gx', 'gy', 'gz')
All inputs are finite; a program needn't handle non-finite values.
Results may differ from a plain program's by a relative error of at most 0.00031.
Values sent between devices are 32-bit elements; how exact they have to be, the bound alone decides.
A program may use at most 64 MiB of HBM per device.

v0:
```python
import jax
import jax.numpy as jnp
from jax import lax
from jax.sharding import PartitionSpec as P

SWEEPS = 4


def with_halo(block, sides, width):
    for axis, dim in sides:
        count = lax.axis_size(axis)
        forward = [(i, i + 1) for i in range(count - 1)]
        backward = [(target, source) for source, target in forward]
        low = lax.ppermute(
            lax.slice_in_dim(block, block.shape[dim] - width, None, axis=dim), axis, forward
        )
        high = lax.ppermute(lax.slice_in_dim(block, 0, width, axis=dim), axis, backward)
        block = jnp.concatenate([low, block, high], axis=dim)
    return block


def prior_root(source, reaction):
    sweeps = SWEEPS
    diagonal = reaction + 6.0
    field = source / diagonal
    for sweep_index in range(sweeps - 1):
        padded = with_halo(field, (("gx", 1), ("gy", 2), ("gz", 3)), 1)
        total = padded[:, 2:, 1:-1, 1:-1] + padded[:, :-2, 1:-1, 1:-1]
        total = total + padded[:, 1:-1, 2:, 1:-1] + padded[:, 1:-1, :-2, 1:-1]
        total = total + padded[:, 1:-1, 1:-1, 2:] + padded[:, 1:-1, 1:-1, :-2]
        field = (source + total) / diagonal
    return field


def body(gradient, noise_draw, current, eigvectors, eigvalues, reaction):
    chains = gradient.shape[0]
    rank = eigvectors.shape[3]
    cells = reaction.shape[0] * reaction.shape[1] * reaction.shape[2]
    basis = eigvectors.reshape(cells, rank)
    stacked = jnp.concatenate(
        [gradient.reshape(chains, cells), noise_draw.reshape(chains, cells)], 0
    )
    partial_sums = jnp.dot(stacked, basis, preferred_element_type=jnp.float32)
    local_part = -0.5 * gradient.astype(jnp.float32) + 1.0 * noise_draw.astype(jnp.float32)
    sums = lax.psum(partial_sums, ("gx", "gy", "gz"))
    damp = eigvalues / (eigvalues + 1.0)
    root_damp = 1.0 - 1.0 / jnp.sqrt(1.0 + eigvalues)
    coef = (0.5 * damp * sums[:chains] - 1.0 * root_damp * sums[chains:]).astype(jnp.bfloat16)
    corr = lax.dot_general(
        coef, basis, (((1,), (1,)), ((), ())), preferred_element_type=jnp.float32
    )
    field = prior_root(local_part + corr.reshape(current.shape), reaction)
    return current + field


def solution(mesh):
    return jax.shard_map(
        body,
        mesh=mesh,
        in_specs=(
            P(None, "gx", "gy", "gz"),
            P(None, "gx", "gy", "gz"),
            P(None, "gx", "gy", "gz"),
            P("gx", "gy", "gz", None),
            P(),
            P("gx", "gy", "gz"),
        ),
        out_specs=P(None, "gx", "gy", "gz"),
        check_vma=False,
    )
```

profile of v0, /device:TPU:0, one launch (start us, length us, event | category | flops | bytes accessed | tf_op | source)
XLA Modules:
  0.0 262.8 jit_solution(8625238853567087662)
XLA Ops:
  8.4 5.7 %fusion.22 = f32[64,512]{1,0:T(8,128)} fusion(bf16[8192,512]{1,0:T(8,128)(2,1)} %bitcast.18, bf16[32,8192]{1,0:T(8,128)(2,1)S(1)} %get-tuple-element.27, bf16[32,8192]{1,0:T(8,128)(2,1)S(1)} %get-tuple-element.28), kind=kOutput, calls=%fused_computation.80 | convolution fusion | flops 538968064 | bytes 9568256 | tf_op jit(solution)/shard_map/dot_general | solution.py:43
  14.2 127.2 %all-reduce.2.cloned.1.call-done = f32[64,512]{1,0:T(8,128)} async-done(((f32[64,512]{1,0:T(8,128)}), f32[64,512]{1,0:T(8,128)}) %all-reduce.2.cloned.1.call-update) | async-done | bytes 131088 | tf_op jit(solution)/shard_map/psum | solution.py:45
  141.5 6.0 %broadcast_divide_fusion = (f32[32,8,8,128]{3,0,2,1:T(8,128)S(1)}, f32[32,8,8,128]{3,0,2,1:T(8,128)S(1)}) fusion(f32[8,8,128]{2,1,0:T(8,128)S(1)} %broadcast_add_fusion, bf16[8,8,128,512]{3,2,1,0:T(8,128)(2,1)} %param.9, f32[64,512]{1,0:T(8,128)} %all-reduce.2.cloned.1.call-done, f32[512]{0:T(512)S(1)} %get-tuple-element.24, f32[512]{0:T(512)S(1)} %get-tuple-element.23, ...), kind=kOutput, calls=%fused_computation.86 | convolution fusion | flops 270073856 | bytes 11702272 | tf_op jit(solution)/shard_map/dot_general | solution.py:49
  147.5 3.4 %collective-permute-start.1 = (f32[32,1,8,128]{3,0,2,1:T(8,128)S(1)}, f32[32,1,8,128]{3,0,2,1:T(8,128)S(1)}, u32[]{:S(2)}, u32[]{:S(2)}) collective-permute-start(f32[32,1,8,128]{3,0,2,1:T(8,128)S(1)} %get-tuple-element.21), channel_id=1, source_target_pairs={{0,8},{8,16},{16,24},{1,9},{9,17},{17,25},{2,10},{10,18},{18,26},{... | collective-permute-start | bytes 393224 | tf_op jit(solution)/shard_map/ppermute | solution.py:14
  153.4 4.7 %collective-permute-done = f32[32,1,8,128]{3,0,2,1:T(8,128)S(1)} collective-permute-done((f32[32,1,8,128]{3,0,2,1:T(8,128)S(1)}, f32[32,1,8,128]{3,0,2,1:T(8,128)S(1)}, u32[]{:S(2)}, u32[]{:S(2)}) %collective-permute-start) | collective-permute-done | bytes 131104 | tf_op jit(solution)/shard_map/ppermute | solution.py:17
  163.4 2.3 fusion.37
  165.7 2.1 copy.13
  169.0 2.1 copy.15
  171.1 4.6 %collective-permute-start.5 = (f32[32,10,10,1]{0,3,2,1:T(1,128)S(1)}, f32[32,10,10,1]{0,3,2,1:T(1,128)S(1)}, u32[]{:S(2)}, u32[]{:S(2)}) collective-permute-start(f32[32,10,10,1]{0,3,2,1:T(1,128)S(1)} %copy.15), channel_id=1, source_target_pairs={{0,1},{1,2},{2,3},{4,5},{5,6},{6,7},{8,9},{9,10},{10,11},{12,13},{... | collective-permute-start | bytes 38408 | tf_op jit(solution)/shard_map/ppermute | solution.py:14
  179.4 2.9 %fusion.17 = f32[32,8,8,128]{3,0,2,1:T(8,128)S(1)} fusion(f32[32,8,8,128]{3,0,2,1:T(8,128)S(1)} %get-tuple-element.26, f32[32,10,10,1]{3,0,2,1:T(8,128)} %copy.16, f32[32,10,1,128]{3,0,2,1:T(8,128)} %copy-done.5, f32[32,10,1,128]{3,0,2,1:T(8,128)} %copy-done.3, f32[32,1,8,128]{3,0,2,1:T(8,128)S(1)} %collective-permute-done, ...), kind=kLoop, calls=%fused_computation.58 | loop fusion | flops 6553600 | bytes 3793920 | tf_op jit(solution)/shard_map/div | solution.py:31
  182.3 3.9 %collective-permute-start.7 = (f32[32,1,8,128]{3,0,2,1:T(8,128)S(1)}, f32[32,1,8,128]{3,0,2,1:T(8,128)S(1)}, u32[]{:S(2)}, u32[]{:S(2)}) collective-permute-start(f32[32,1,8,128]{3,0,2,1:T(8,128)S(1)} %get-tuple-element.19), channel_id=1, source_target_pairs={{0,8},{8,16},{16,24},{1,9},{9,17},{17,25},{2,10},{10,18},{18,26},{... | collective-permute-start | bytes 393224 | tf_op jit(solution)/shard_map/ppermute | solution.py:14
  188.8 4.4 %collective-permute-done.6 = f32[32,1,8,128]{3,0,2,1:T(8,128)S(1)} collective-permute-done((f32[32,1,8,128]{3,0,2,1:T(8,128)S(1)}, f32[32,1,8,128]{3,0,2,1:T(8,128)S(1)}, u32[]{:S(2)}, u32[]{:S(2)}) %collective-permute-start.6) | collective-permute-done | bytes 131104 | tf_op jit(solution)/shard_map/ppermute | solution.py:17
  198.4 2.3 fusion.36
  200.7 2.1 copy.17
  204.0 2.1 copy.19
  206.1 4.8 %collective-permute-start.11 = (f32[32,10,10,1]{0,3,2,1:T(1,128)S(1)}, f32[32,10,10,1]{0,3,2,1:T(1,128)S(1)}, u32[]{:S(2)}, u32[]{:S(2)}) collective-permute-start(f32[32,10,10,1]{0,3,2,1:T(1,128)S(1)} %copy.19), channel_id=1, source_target_pairs={{0,1},{1,2},{2,3},{4,5},{5,6},{6,7},{8,9},{9,10},{10,11},{12,13},{... | collective-permute-start | bytes 38408 | tf_op jit(solution)/shard_map/ppermute | solution.py:14
  214.6 2.9 %fusion.10 = f32[32,8,8,128]{3,0,2,1:T(8,128)S(1)} fusion(f32[32,8,8,128]{3,0,2,1:T(8,128)S(1)} %get-tuple-element.26, f32[32,10,10,1]{3,0,2,1:T(8,128)} %copy.20, f32[32,10,1,128]{3,0,2,1:T(8,128)} %copy-done.6, f32[32,10,1,128]{3,0,2,1:T(8,128)} %copy-done.4, f32[32,1,8,128]{3,0,2,1:T(8,128)S(1)} %collective-permute-done.6, ...), kind=kLoop, calls=%fused_computation.33 | loop fusion | flops 6553600 | bytes 3793920 | tf_op jit(solution)/shard_map/div | solution.py:31
  217.5 3.4 %collective-permute-start.13 = (f32[32,1,8,128]{3,0,2,1:T(8,128)S(1)}, f32[32,1,8,128]{3,0,2,1:T(8,128)S(1)}, u32[]{:S(2)}, u32[]{:S(2)}) collective-permute-start(f32[32,1,8,128]{3,0,2,1:T(8,128)S(1)} %get-tuple-element.17), channel_id=1, source_target_pairs={{0,8},{8,16},{16,24},{1,9},{9,17},{17,25},{2,10},{10,18},{18,26},{... | collective-permute-start | bytes 393224 | tf_op jit(solution)/shard_map/ppermute | solution.py:14
  223.7 4.1 %collective-permute-done.12 = f32[32,1,8,128]{3,0,2,1:T(8,128)S(1)} collective-permute-done((f32[32,1,8,128]{3,0,2,1:T(8,128)S(1)}, f32[32,1,8,128]{3,0,2,1:T(8,128)S(1)}, u32[]{:S(2)}, u32[]{:S(2)}) %collective-permute-start.12) | collective-permute-done | bytes 131104 | tf_op jit(solution)/shard_map/ppermute | solution.py:17
  233.1 2.2 fusion.35
  238.7 2.7 %copy.23 = f32[32,10,10,1]{0,3,2,1:T(1,128)} copy(f32[32,10,10,1]{3,0,2,1:T(8,128)} %get-tuple-element.6) | data formatting | bytes 25600 | tf_op jit(solution)/shard_map/slice | solution.py:15
  241.4 5.5 %collective-permute-start.17 = (f32[32,10,10,1]{0,3,2,1:T(1,128)}, f32[32,10,10,1]{0,3,2,1:T(1,128)}, u32[]{:S(2)}, u32[]{:S(2)}) collective-permute-start(f32[32,10,10,1]{0,3,2,1:T(1,128)} %copy.23), channel_id=1, source_target_pairs={{0,1},{1,2},{2,3},{4,5},{5,6},{6,7},{8,9},{9,10},{10,11},{12,13},{... | collective-permute-start | bytes 38408 | tf_op jit(solution)/shard_map/ppermute | solution.py:14
  248.8 2.6 %copy.24 = f32[32,10,10,1]{3,0,2,1:T(8,128)} copy(f32[32,10,10,1]{0,3,2,1:T(1,128)} %collective-permute-done.17) | data formatting | bytes 25600 | tf_op jit(solution)/shard_map/ppermute | solution.py:14
  251.4 3.0 %fusion.3 = f32[32,8,8,128]{3,0,2,1:T(8,128)S(1)} fusion(f32[32,8,8,128]{3,0,2,1:T(8,128)S(1)} %get-tuple-element.26, f32[32,10,10,1]{3,0,2,1:T(8,128)} %copy.24, f32[32,10,1,128]{3,0,2,1:T(8,128)} %copy-done.8, f32[32,10,1,128]{3,0,2,1:T(8,128)} %copy-done.7, f32[32,1,8,128]{3,0,2,1:T(8,128)S(1)} %collective-permute-done.12, ...), kind=kLoop, calls=%fused_computation.8 | loop fusion | flops 6815744 | bytes 4842496 | tf_op jit(solution)/shard_map/add | solution.py:53
  (70 shorter events, 42.2 us)
Async XLA Ops:
  6.5 134.9 %all-reduce.2.cloned.1.call-start = ((), (), s32[]{:S(2)}) async-start(), calls=%async_computation | async-start | bytes 262144 | tf_op jit(solution)/shard_map/psum | solution.py:45
  8.4 5.8 %copy-start.9 = (f32[8,8,128]{2,1,0:T(8,128)S(1)}, f32[8,8,128]{2,1,0:T(8,128)}, u32[]{:S(2)}) copy-start(f32[8,8,128]{2,1,0:T(8,128)} %param.11) | copy-start | bytes 98308
  8.4 5.8 %copy-start.10 = (f32[512]{0:T(512)S(1)}, f32[512]{0:T(512)}, u32[]{:S(2)}) copy-start(f32[512]{0:T(512)} %param.10) | copy-start | bytes 6148
  8.4 133.0 %copy-start = (bf16[32,8,8,128]{3,2,1,0:T(8,128)(2,1)S(1)}, bf16[32,8,8,128]{3,2,1,0:T(8,128)(2,1)}, u32[]{:S(2)}) copy-start(bf16[32,8,8,128]{3,2,1,0:T(8,128)(2,1)} %param.7) | copy-start | bytes 1572868
  8.4 133.0 %copy-start.1 = (bf16[32,8,8,128]{3,2,1,0:T(8,128)(2,1)S(1)}, bf16[32,8,8,128]{3,2,1,0:T(8,128)(2,1)}, u32[]{:S(2)}) copy-start(bf16[32,8,8,128]{3,2,1,0:T(8,128)(2,1)} %param.6) | copy-start | bytes 1572868
  147.5 5.9 %collective-permute-start.1 = (f32[32,1,8,128]{3,0,2,1:T(8,128)S(1)}, f32[32,1,8,128]{3,0,2,1:T(8,128)S(1)}, u32[]{:S(2)}, u32[]{:S(2)}) collective-permute-start(f32[32,1,8,128]{3,0,2,1:T(8,128)S(1)} %get-tuple-element.21), channel_id=1, source_target_pairs={{0,8},{8,16},{16,24},{1,9},{9,17},{17,25},{2,10},{10,18},{18,26},{... | collective-permute-start | bytes 393224 | tf_op jit(solution)/shard_map/ppermute | solution.py:14
  150.9 7.2 %collective-permute-start = (f32[32,1,8,128]{3,0,2,1:T(8,128)S(1)}, f32[32,1,8,128]{3,0,2,1:T(8,128)S(1)}, u32[]{:S(2)}, u32[]{:S(2)}) collective-permute-start(f32[32,1,8,128]{3,0,2,1:T(8,128)S(1)} %get-tuple-element.22), channel_id=1, source_target_pairs={{8,0},{16,8},{24,16},{9,1},{17,9},{25,17},{10,2},{18,10},{26,18},{... | collective-permute-start | bytes 393224 | tf_op jit(solution)/shard_map/ppermute | solution.py:17
  158.1 2.6 collective-permute-start.3
  159.5 3.3 %collective-permute-start.2 = (f32[32,10,1,128]{3,0,2,1:T(8,128)S(1)}, f32[32,10,1,128]{3,0,2,1:T(8,128)S(1)}, u32[]{:S(2)}, u32[]{:S(2)}) collective-permute-start(f32[32,10,1,128]{3,0,2,1:T(8,128)S(1)} %get-tuple-element.16), channel_id=1, source_target_pairs={{4,0},{5,1},{6,2},{7,3},{12,8},{13,9},{14,10},{15,11},{20,16},{21,... | collective-permute-start | bytes 491528 | tf_op jit(solution)/shard_map/ppermute | solution.py:17
  167.7 7.9 %collective-permute-start.4 = (f32[32,10,10,1]{0,3,2,1:T(1,128)S(1)}, f32[32,10,10,1]{0,3,2,1:T(1,128)S(1)}, u32[]{:S(2)}, u32[]{:S(2)}) collective-permute-start(f32[32,10,10,1]{0,3,2,1:T(1,128)S(1)} %copy.13), channel_id=1, source_target_pairs={{1,0},{2,1},{3,2},{5,4},{6,5},{7,6},{9,8},{10,9},{11,10},{13,12},{... | collective-permute-start | bytes 38408 | tf_op jit(solution)/shard_map/ppermute | solution.py:17
  171.1 6.4 %collective-permute-start.5 = (f32[32,10,10,1]{0,3,2,1:T(1,128)S(1)}, f32[32,10,10,1]{0,3,2,1:T(1,128)S(1)}, u32[]{:S(2)}, u32[]{:S(2)}) collective-permute-start(f32[32,10,10,1]{0,3,2,1:T(1,128)S(1)} %copy.15), channel_id=1, source_target_pairs={{0,1},{1,2},{2,3},{4,5},{5,6},{6,7},{8,9},{9,10},{10,11},{12,13},{... | collective-permute-start | bytes 38408 | tf_op jit(solution)/shard_map/ppermute | solution.py:14
  182.3 6.4 %collective-permute-start.7 = (f32[32,1,8,128]{3,0,2,1:T(8,128)S(1)}, f32[32,1,8,128]{3,0,2,1:T(8,128)S(1)}, u32[]{:S(2)}, u32[]{:S(2)}) collective-permute-start(f32[32,1,8,128]{3,0,2,1:T(8,128)S(1)} %get-tuple-element.19), channel_id=1, source_target_pairs={{0,8},{8,16},{16,24},{1,9},{9,17},{17,25},{2,10},{10,18},{18,26},{... | collective-permute-start | bytes 393224 | tf_op jit(solution)/shard_map/ppermute | solution.py:14
  186.3 6.9 %collective-permute-start.6 = (f32[32,1,8,128]{3,0,2,1:T(8,128)S(1)}, f32[32,1,8,128]{3,0,2,1:T(8,128)S(1)}, u32[]{:S(2)}, u32[]{:S(2)}) collective-permute-start(f32[32,1,8,128]{3,0,2,1:T(8,128)S(1)} %get-tuple-element.20), channel_id=1, source_target_pairs={{8,0},{16,8},{24,16},{9,1},{17,9},{25,17},{10,2},{18,10},{26,18},{... | collective-permute-start | bytes 393224 | tf_op jit(solution)/shard_map/ppermute | solution.py:17
  193.2 2.6 collective-permute-start.9
  194.5 3.3 %collective-permute-start.8 = (f32[32,10,1,128]{3,0,2,1:T(8,128)S(1)}, f32[32,10,1,128]{3,0,2,1:T(8,128)S(1)}, u32[]{:S(2)}, u32[]{:S(2)}) collective-permute-start(f32[32,10,1,128]{3,0,2,1:T(8,128)S(1)} %get-tuple-element.14), channel_id=1, source_target_pairs={{4,0},{5,1},{6,2},{7,3},{12,8},{13,9},{14,10},{15,11},{20,16},{21,... | collective-permute-start | bytes 491528 | tf_op jit(solution)/shard_map/ppermute | solution.py:17
  202.7 8.2 %collective-permute-start.10 = (f32[32,10,10,1]{0,3,2,1:T(1,128)S(1)}, f32[32,10,10,1]{0,3,2,1:T(1,128)S(1)}, u32[]{:S(2)}, u32[]{:S(2)}) collective-permute-start(f32[32,10,10,1]{0,3,2,1:T(1,128)S(1)} %copy.17), channel_id=1, source_target_pairs={{1,0},{2,1},{3,2},{5,4},{6,5},{7,6},{9,8},{10,9},{11,10},{13,12},{... | collective-permute-start | bytes 38408 | tf_op jit(solution)/shard_map/ppermute | solution.py:17
  206.1 6.6 %collective-permute-start.11 = (f32[32,10,10,1]{0,3,2,1:T(1,128)S(1)}, f32[32,10,10,1]{0,3,2,1:T(1,128)S(1)}, u32[]{:S(2)}, u32[]{:S(2)}) collective-permute-start(f32[32,10,10,1]{0,3,2,1:T(1,128)S(1)} %copy.19), channel_id=1, source_target_pairs={{0,1},{1,2},{2,3},{4,5},{5,6},{6,7},{8,9},{9,10},{10,11},{12,13},{... | collective-permute-start | bytes 38408 | tf_op jit(solution)/shard_map/ppermute | solution.py:14
  217.5 6.1 %collective-permute-start.13 = (f32[32,1,8,128]{3,0,2,1:T(8,128)S(1)}, f32[32,1,8,128]{3,0,2,1:T(8,128)S(1)}, u32[]{:S(2)}, u32[]{:S(2)}) collective-permute-start(f32[32,1,8,128]{3,0,2,1:T(8,128)S(1)} %get-tuple-element.17), channel_id=1, source_target_pairs={{0,8},{8,16},{16,24},{1,9},{9,17},{17,25},{2,10},{10,18},{18,26},{... | collective-permute-start | bytes 393224 | tf_op jit(solution)/shard_map/ppermute | solution.py:14
  220.9 6.9 %collective-permute-start.12 = (f32[32,1,8,128]{3,0,2,1:T(8,128)S(1)}, f32[32,1,8,128]{3,0,2,1:T(8,128)S(1)}, u32[]{:S(2)}, u32[]{:S(2)}) collective-permute-start(f32[32,1,8,128]{3,0,2,1:T(8,128)S(1)} %get-tuple-element.18), channel_id=1, source_target_pairs={{8,0},{16,8},{24,16},{9,1},{17,9},{25,17},{10,2},{18,10},{26,18},{... | collective-permute-start | bytes 393224 | tf_op jit(solution)/shard_map/ppermute | solution.py:17
  227.8 2.6 collective-permute-start.15
  229.1 3.3 %collective-permute-start.14 = (f32[32,10,1,128]{3,0,2,1:T(8,128)S(1)}, f32[32,10,1,128]{3,0,2,1:T(8,128)S(1)}, u32[]{:S(2)}, u32[]{:S(2)}) collective-permute-start(f32[32,10,1,128]{3,0,2,1:T(8,128)S(1)} %get-tuple-element.12), channel_id=1, source_target_pairs={{4,0},{5,1},{6,2},{7,3},{12,8},{13,9},{14,10},{15,11},{20,16},{21,... | collective-permute-start | bytes 491528 | tf_op jit(solution)/shard_map/ppermute | solution.py:17
  237.4 9.5 %collective-permute-start.16 = (f32[32,10,10,1]{0,3,2,1:T(1,128)S(1)}, f32[32,10,10,1]{0,3,2,1:T(1,128)S(1)}, u32[]{:S(2)}, u32[]{:S(2)}) collective-permute-start(f32[32,10,10,1]{0,3,2,1:T(1,128)S(1)} %copy.21), channel_id=1, source_target_pairs={{1,0},{2,1},{3,2},{5,4},{6,5},{7,6},{9,8},{10,9},{11,10},{13,12},{... | collective-permute-start | bytes 38408 | tf_op jit(solution)/shard_map/ppermute | solution.py:17
  241.4 10.0 %copy-start.2 = (f32[32,8,8,128]{3,2,1,0:T(8,128)S(1)}, f32[32,8,8,128]{3,2,1,0:T(8,128)}, u32[]{:S(2)}) copy-start(f32[32,8,8,128]{3,2,1,0:T(8,128)} %param.8) | copy-start | bytes 3145732
  241.4 7.4 %collective-permute-start.17 = (f32[32,10,10,1]{0,3,2,1:T(1,128)}, f32[32,10,10,1]{0,3,2,1:T(1,128)}, u32[]{:S(2)}, u32[]{:S(2)}) collective-permute-start(f32[32,10,10,1]{0,3,2,1:T(1,128)} %copy.23), channel_id=1, source_target_pairs={{0,1},{1,2},{2,3},{4,5},{5,6},{6,7},{8,9},{9,10},{10,11},{12,13},{... | collective-permute-start | bytes 38408 | tf_op jit(solution)/shard_map/ppermute | solution.py:14
  (6 other events, 8.5 us)
Sparse Core Ops, SparseCore 0:
  14.3 127.1 all-reduce.1
where the time goes:
time: 264 us; the launch traced here: 263 us
  waiting for transfers between devices  150 us (57%)
  starting transfers between devices  41.1 us (16%)
  local copies, waits for them, and re-layouts  36.7 us (14%)
  between operations  13.8 us (5%)
  matrix products  11.7 us (4%)
  other arithmetic  9.37 us (4%)
    psum x1, waiting for transfers between devices, body(): sums = lax.psum(partial_sums, ('gx', 'gy', 'gz'))  127 us
    ppermute x9, starting transfers between devices, with_halo(): lax.ppermute(lax.slice_in_dim(block, block.shape[dim] - width, None, axis...  29.4 us
    ppermute x9, waiting for transfers between devices, with_halo(): lax.ppermute(lax.slice_in_dim(block, 0, width, axis=dim), axis, backward)  19.1 us
    slice x6, local copies, waits for them, and re-layouts, with_halo(): lax.slice_in_dim(block, 0, width, axis=dim)  13 us
    ppermute x9, starting transfers between devices, with_halo(): lax.ppermute(lax.slice_in_dim(block, 0, width, axis=dim), axis, backward)  11.6 us
    slice x6, local copies, waits for them, and re-layouts, with_halo(): lax.slice_in_dim(block, block.shape[dim] - width, None, axis=dim)  6.9 us
    ppermute x3, local copies, waits for them, and re-layouts, with_halo(): lax.ppermute(lax.slice_in_dim(block, block.shape[dim] - width, None, axis...  6.34 us
    dot_general x1, matrix products, body(): lax.dot_general(coef, basis, (((1,), (1,)), ((), ())), preferred_element_...  6.04 us
  transfers between devices with their start and end apart: 19, of which 10 were waited for; matrix products, arithmetic and copies ran while one was open for 5% of the time, Pallas kernels for 0%

commit v1 on v0

--- a/solution.py
+++ b/solution.py
@@ -42,7 +42,7 @@
     )
     partial_sums = jnp.dot(stacked, basis, preferred_element_type=jnp.float32)
     local_part = -0.5 * gradient.astype(jnp.float32) + 1.0 * noise_draw.astype(jnp.float32)
-    sums = lax.psum(partial_sums, ("gx", "gy", "gz"))
+    sums = jnp.sum(lax.all_gather(partial_sums, ("gx", "gy", "gz")), axis=0)
     damp = eigvalues / (eigvalues + 1.0)
     root_damp = 1.0 - 1.0 / jnp.sqrt(1.0 + eigvalues)
     coef = (0.5 * damp * sums[:chains] - 1.0 * root_damp * sums[chains:]).astype(jnp.bfloat16)

time: 264 us -> 204 us (0.77)
  waiting for transfers between devices: 150 us -> 88.3 us
    psum x1 -> x0, waiting for transfers between devices: 127 us -> none  [body(): sums = lax.psum(partial_sums, ('gx', 'gy', 'gz'))]
    all_gather x0 -> x1, waiting for transfers between devices: none -> 64.5 us  [body(): sums = jnp.sum(lax.all_gather(partial_sums, ('gx', 'gy', 'gz')), axis=0)]
  transfers between devices with their start and end apart: 19 -> 19, of which waited for: 10 -> 10; matrix products, arithmetic and copies ran while one was open for 5% -> 6% of each run, Pallas kernels for 0% -> 0%
where the time goes in v1:
time: 204 us; the launch traced here: 203 us
  waiting for transfers between devices  88.3 us (43%)
  starting transfers between devices  40.2 us (20%)
  local copies, waits for them, and re-layouts  36.8 us (18%)
  between operations  13.8 us (7%)
  other arithmetic  12 us (6%)
  matrix products  11.6 us (6%)
    all_gather x1, waiting for transfers between devices, body(): sums = jnp.sum(lax.all_gather(partial_sums, ('gx', 'gy', 'gz')), axis=0)  64.5 us
    ppermute x9, starting transfers between devices, with_halo(): lax.ppermute(lax.slice_in_dim(block, block.shape[dim] - width, None, axis...  28.4 us
    ppermute x9, waiting for transfers between devices, with_halo(): lax.ppermute(lax.slice_in_dim(block, 0, width, axis=dim), axis, backward)  19.3 us
    slice x6, local copies, waits for them, and re-layouts, with_halo(): lax.slice_in_dim(block, 0, width, axis=dim)  13 us
    ppermute x9, starting transfers between devices, with_halo(): lax.ppermute(lax.slice_in_dim(block, 0, width, axis=dim), axis, backward)  11.8 us
    slice x6, local copies, waits for them, and re-layouts, with_halo(): lax.slice_in_dim(block, block.shape[dim] - width, None, axis=dim)  6.9 us
    ppermute x3, local copies, waits for them, and re-layouts, with_halo(): lax.ppermute(lax.slice_in_dim(block, block.shape[dim] - width, None, axis...  6.34 us
    dot_general x1, matrix products, body(): lax.dot_general(coef, basis, (((1,), (1,)), ((), ())), preferred_element_...  5.97 us
  transfers between devices with their start and end apart: 19, of which 10 were waited for; matrix products, arithmetic and copies ran while one was open for 6% of the time, Pallas kernels for 0%

profile of v1, /device:TPU:0, one launch (start us, length us, event | category | flops | bytes accessed | tf_op | source)
XLA Modules:
  0.0 202.7 jit_solution(388564324414151335)
XLA Ops:
  8.4 5.6 %fusion.22 = f32[64,512]{1,0:T(8,128)} fusion(bf16[8192,512]{1,0:T(8,128)(2,1)} %bitcast.19, bf16[32,8192]{1,0:T(8,128)(2,1)S(1)} %get-tuple-element.27, bf16[32,8192]{1,0:T(8,128)(2,1)S(1)} %get-tuple-element.28), kind=kOutput, calls=%fused_computation.80 | convolution fusion | flops 538968064 | bytes 9568256 | tf_op jit(solution)/shard_map/dot_general | solution.py:43
  14.1 64.5 %all-gather.3.cloned.1.call-done = f32[2048,512]{1,0:T(8,128)} async-done(((f32[64,512]{1,0:T(8,128)}), f32[2048,512]{1,0:T(8,128)}) %all-gather.3.cloned.1.call-update) | async-done | bytes 4194320 | tf_op jit(solution)/shard_map/all_gather | solution.py:45
  78.6 2.6 %reduce_sum.9 = f32[64,512]{1,0:T(8,128)S(1)} reduce(f32[32,64,512]{2,1,0:T(8,128)} %bitcast.20, f32[]{:T(128)} %constant.3.clone.1), dimensions={0}, to_apply=%region_0.0 | reduce | flops 1015808 | bytes 4325380 | tf_op jit(solution)/shard_map/reduce_sum | solution.py:45
  81.2 6.0 %broadcast_divide_fusion = (f32[32,8,8,128]{3,0,2,1:T(8,128)S(1)}, f32[32,8,8,128]{3,0,2,1:T(8,128)S(1)}) fusion(f32[8,8,128]{2,1,0:T(8,128)S(1)} %broadcast_add_fusion, bf16[8,8,128,512]{3,2,1,0:T(8,128)(2,1)} %param.9, f32[64,512]{1,0:T(8,128)S(1)} %reduce_sum.9, f32[512]{0:T(512)S(1)} %get-tuple-element.24, f32[512]{0:T(512)S(1)} %get-tuple-element.23, ...), kind=kOutput, calls=%fused_computation.86 | convolution fusion | flops 270073856 | bytes 11702272 | tf_op jit(solution)/shard_map/dot_general | solution.py:49
  87.2 3.2 %collective-permute-start.1 = (f32[32,1,8,128]{3,0,2,1:T(8,128)S(1)}, f32[32,1,8,128]{3,0,2,1:T(8,128)S(1)}, u32[]{:S(2)}, u32[]{:S(2)}) collective-permute-start(f32[32,1,8,128]{3,0,2,1:T(8,128)S(1)} %get-tuple-element.21), channel_id=1, source_target_pairs={{0,8},{8,16},{16,24},{1,9},{9,17},{17,25},{2,10},{10,18},{18,26},{... | collective-permute-start | bytes 393224 | tf_op jit(solution)/shard_map/ppermute | solution.py:14
  93.5 4.9 %collective-permute-done = f32[32,1,8,128]{3,0,2,1:T(8,128)S(1)} collective-permute-done((f32[32,1,8,128]{3,0,2,1:T(8,128)S(1)}, f32[32,1,8,128]{3,0,2,1:T(8,128)S(1)}, u32[]{:S(2)}, u32[]{:S(2)}) %collective-permute-start) | collective-permute-done | bytes 131104 | tf_op jit(solution)/shard_map/ppermute | solution.py:17
  103.8 2.3 %fusion.37 = (f32[32,10,10,1]{3,0,2,1:T(8,128)}, f32[32,10,10,1]{3,0,2,1:T(8,128)}) fusion(f32[32,10,10,128]{3,0,2,1:T(8,128)S(1)} %pad_maximum_fusion), kind=kLoop, calls=%fused_computation.111 | loop fusion | bytes 51200 | tf_op jit(solution)/shard_map/slice | solution.py:17
  106.0 2.1 %copy.13 = f32[32,10,10,1]{0,3,2,1:T(1,128)S(1)} copy(f32[32,10,10,1]{3,0,2,1:T(8,128)} %get-tuple-element.9) | data formatting | bytes 25600 | tf_op jit(solution)/shard_map/slice | solution.py:17
  109.4 2.1 %copy.15 = f32[32,10,10,1]{0,3,2,1:T(1,128)S(1)} copy(f32[32,10,10,1]{3,0,2,1:T(8,128)} %get-tuple-element.10) | data formatting | bytes 25600 | tf_op jit(solution)/shard_map/slice | solution.py:15
  111.5 4.6 %collective-permute-start.5 = (f32[32,10,10,1]{0,3,2,1:T(1,128)S(1)}, f32[32,10,10,1]{0,3,2,1:T(1,128)S(1)}, u32[]{:S(2)}, u32[]{:S(2)}) collective-permute-start(f32[32,10,10,1]{0,3,2,1:T(1,128)S(1)} %copy.15), channel_id=1, source_target_pairs={{0,1},{1,2},{2,3},{4,5},{5,6},{6,7},{8,9},{9,10},{10,11},{12,13},{... | collective-permute-start | bytes 38408 | tf_op jit(solution)/shard_map/ppermute | solution.py:14
  119.7 2.9 %fusion.17 = f32[32,8,8,128]{3,0,2,1:T(8,128)S(1)} fusion(f32[32,8,8,128]{3,0,2,1:T(8,128)S(1)} %get-tuple-element.26, f32[32,10,10,1]{3,0,2,1:T(8,128)} %copy.16, f32[32,10,1,128]{3,0,2,1:T(8,128)} %copy-done.5, f32[32,10,1,128]{3,0,2,1:T(8,128)} %copy-done.3, f32[32,1,8,128]{3,0,2,1:T(8,128)S(1)} %collective-permute-done, ...), kind=kLoop, calls=%fused_computation.58 | loop fusion | flops 6553600 | bytes 3793920 | tf_op jit(solution)/shard_map/div | solution.py:31
  122.7 3.7 %collective-permute-start.7 = (f32[32,1,8,128]{3,0,2,1:T(8,128)S(1)}, f32[32,1,8,128]{3,0,2,1:T(8,128)S(1)}, u32[]{:S(2)}, u32[]{:S(2)}) collective-permute-start(f32[32,1,8,128]{3,0,2,1:T(8,128)S(1)} %get-tuple-element.19), channel_id=1, source_target_pairs={{0,8},{8,16},{16,24},{1,9},{9,17},{17,25},{2,10},{10,18},{18,26},{... | collective-permute-start | bytes 393224 | tf_op jit(solution)/shard_map/ppermute | solution.py:14
  128.8 4.4 %collective-permute-done.6 = f32[32,1,8,128]{3,0,2,1:T(8,128)S(1)} collective-permute-done((f32[32,1,8,128]{3,0,2,1:T(8,128)S(1)}, f32[32,1,8,128]{3,0,2,1:T(8,128)S(1)}, u32[]{:S(2)}, u32[]{:S(2)}) %collective-permute-start.6) | collective-permute-done | bytes 131104 | tf_op jit(solution)/shard_map/ppermute | solution.py:17
  138.7 2.3 %fusion.36 = (f32[32,10,10,1]{3,0,2,1:T(8,128)}, f32[32,10,10,1]{3,0,2,1:T(8,128)}) fusion(f32[32,10,10,128]{3,0,2,1:T(8,128)S(1)} %pad_maximum_fusion.1), kind=kLoop, calls=%fused_computation.110 | loop fusion | bytes 51200 | tf_op jit(solution)/shard_map/slice | solution.py:17
  144.3 2.1 %copy.19 = f32[32,10,10,1]{0,3,2,1:T(1,128)S(1)} copy(f32[32,10,10,1]{3,0,2,1:T(8,128)} %get-tuple-element.8) | data formatting | bytes 25600 | tf_op jit(solution)/shard_map/slice | solution.py:15
  146.4 4.8 %collective-permute-start.11 = (f32[32,10,10,1]{0,3,2,1:T(1,128)S(1)}, f32[32,10,10,1]{0,3,2,1:T(1,128)S(1)}, u32[]{:S(2)}, u32[]{:S(2)}) collective-permute-start(f32[32,10,10,1]{0,3,2,1:T(1,128)S(1)} %copy.19), channel_id=1, source_target_pairs={{0,1},{1,2},{2,3},{4,5},{5,6},{6,7},{8,9},{9,10},{10,11},{12,13},{... | collective-permute-start | bytes 38408 | tf_op jit(solution)/shard_map/ppermute | solution.py:14
  154.9 2.9 %fusion.10 = f32[32,8,8,128]{3,0,2,1:T(8,128)S(1)} fusion(f32[32,8,8,128]{3,0,2,1:T(8,128)S(1)} %get-tuple-element.26, f32[32,10,10,1]{3,0,2,1:T(8,128)} %copy.20, f32[32,10,1,128]{3,0,2,1:T(8,128)} %copy-done.6, f32[32,10,1,128]{3,0,2,1:T(8,128)} %copy-done.4, f32[32,1,8,128]{3,0,2,1:T(8,128)S(1)} %collective-permute-done.6, ...), kind=kLoop, calls=%fused_computation.33 | loop fusion | flops 6553600 | bytes 3793920 | tf_op jit(solution)/shard_map/div | solution.py:31
  157.8 2.8 %collective-permute-start.13 = (f32[32,1,8,128]{3,0,2,1:T(8,128)S(1)}, f32[32,1,8,128]{3,0,2,1:T(8,128)S(1)}, u32[]{:S(2)}, u32[]{:S(2)}) collective-permute-start(f32[32,1,8,128]{3,0,2,1:T(8,128)S(1)} %get-tuple-element.17), channel_id=1, source_target_pairs={{0,8},{8,16},{16,24},{1,9},{9,17},{17,25},{2,10},{10,18},{18,26},{... | collective-permute-start | bytes 393224 | tf_op jit(solution)/shard_map/ppermute | solution.py:14
  163.4 4.1 %collective-permute-done.12 = f32[32,1,8,128]{3,0,2,1:T(8,128)S(1)} collective-permute-done((f32[32,1,8,128]{3,0,2,1:T(8,128)S(1)}, f32[32,1,8,128]{3,0,2,1:T(8,128)S(1)}, u32[]{:S(2)}, u32[]{:S(2)}) %collective-permute-start.12) | collective-permute-done | bytes 131104 | tf_op jit(solution)/shard_map/ppermute | solution.py:17
  172.8 2.2 %fusion.35 = (f32[32,10,10,1]{3,0,2,1:T(8,128)}, f32[32,10,10,1]{3,0,2,1:T(8,128)}) fusion(f32[32,10,10,128]{3,0,2,1:T(8,128)S(1)} %pad_maximum_fusion.2), kind=kLoop, calls=%fused_computation.109 | loop fusion | bytes 51200 | tf_op jit(solution)/shard_map/slice | solution.py:17
  178.6 2.7 %copy.23 = f32[32,10,10,1]{0,3,2,1:T(1,128)} copy(f32[32,10,10,1]{3,0,2,1:T(8,128)} %get-tuple-element.6) | data formatting | bytes 25600 | tf_op jit(solution)/shard_map/slice | solution.py:15
  181.3 5.5 %collective-permute-start.17 = (f32[32,10,10,1]{0,3,2,1:T(1,128)}, f32[32,10,10,1]{0,3,2,1:T(1,128)}, u32[]{:S(2)}, u32[]{:S(2)}) collective-permute-start(f32[32,10,10,1]{0,3,2,1:T(1,128)} %copy.23), channel_id=1, source_target_pairs={{0,1},{1,2},{2,3},{4,5},{5,6},{6,7},{8,9},{9,10},{10,11},{12,13},{... | collective-permute-start | bytes 38408 | tf_op jit(solution)/shard_map/ppermute | solution.py:14
  188.7 2.6 %copy.24 = f32[32,10,10,1]{3,0,2,1:T(8,128)} copy(f32[32,10,10,1]{0,3,2,1:T(1,128)} %collective-permute-done.17) | data formatting | bytes 25600 | tf_op jit(solution)/shard_map/ppermute | solution.py:14
  191.3 3.0 %fusion.3 = f32[32,8,8,128]{3,0,2,1:T(8,128)S(1)} fusion(f32[32,8,8,128]{3,0,2,1:T(8,128)S(1)} %get-tuple-element.26, f32[32,10,10,1]{3,0,2,1:T(8,128)} %copy.24, f32[32,10,1,128]{3,0,2,1:T(8,128)} %copy-done.8, f32[32,10,1,128]{3,0,2,1:T(8,128)} %copy-done.7, f32[32,1,8,128]{3,0,2,1:T(8,128)S(1)} %collective-permute-done.12, ...), kind=kLoop, calls=%fused_computation.8 | loop fusion | flops 6815744 | bytes 4842496 | tf_op jit(solution)/shard_map/add | solution.py:53
  (71 shorter events, 45.3 us)
Async XLA Ops:
  6.5 72.0 %all-gather.3.cloned.1.call-start = ((), (), s32[]{:S(2)}) async-start(), calls=%async_computation | async-start | bytes 4325376 | tf_op jit(solution)/shard_map/all_gather | solution.py:45
  8.4 5.7 %copy-start.10 = (f32[512]{0:T(512)S(1)}, f32[512]{0:T(512)}, u32[]{:S(2)}) copy-start(f32[512]{0:T(512)} %param.10) | copy-start | bytes 6148
  8.4 5.7 %copy-start.9 = (f32[8,8,128]{2,1,0:T(8,128)S(1)}, f32[8,8,128]{2,1,0:T(8,128)}, u32[]{:S(2)}) copy-start(f32[8,8,128]{2,1,0:T(8,128)} %param.11) | copy-start | bytes 98308
  78.6 2.6 %copy-start = (bf16[32,8,8,128]{3,2,1,0:T(8,128)(2,1)S(1)}, bf16[32,8,8,128]{3,2,1,0:T(8,128)(2,1)}, u32[]{:S(2)}) copy-start(bf16[32,8,8,128]{3,2,1,0:T(8,128)(2,1)} %param.7) | copy-start | bytes 1572868
  78.6 2.6 %copy-start.1 = (bf16[32,8,8,128]{3,2,1,0:T(8,128)(2,1)S(1)}, bf16[32,8,8,128]{3,2,1,0:T(8,128)(2,1)}, u32[]{:S(2)}) copy-start(bf16[32,8,8,128]{3,2,1,0:T(8,128)(2,1)} %param.6) | copy-start | bytes 1572868
  87.2 6.3 %collective-permute-start.1 = (f32[32,1,8,128]{3,0,2,1:T(8,128)S(1)}, f32[32,1,8,128]{3,0,2,1:T(8,128)S(1)}, u32[]{:S(2)}, u32[]{:S(2)}) collective-permute-start(f32[32,1,8,128]{3,0,2,1:T(8,128)S(1)} %get-tuple-element.21), channel_id=1, source_target_pairs={{0,8},{8,16},{16,24},{1,9},{9,17},{17,25},{2,10},{10,18},{18,26},{... | collective-permute-start | bytes 393224 | tf_op jit(solution)/shard_map/ppermute | solution.py:14
  90.4 8.1 %collective-permute-start = (f32[32,1,8,128]{3,0,2,1:T(8,128)S(1)}, f32[32,1,8,128]{3,0,2,1:T(8,128)S(1)}, u32[]{:S(2)}, u32[]{:S(2)}) collective-permute-start(f32[32,1,8,128]{3,0,2,1:T(8,128)S(1)} %get-tuple-element.22), channel_id=1, source_target_pairs={{8,0},{16,8},{24,16},{9,1},{17,9},{25,17},{10,2},{18,10},{26,18},{... | collective-permute-start | bytes 393224 | tf_op jit(solution)/shard_map/ppermute | solution.py:17
  98.5 2.6 %collective-permute-start.3 = (f32[32,10,1,128]{3,0,2,1:T(8,128)S(1)}, f32[32,10,1,128]{3,0,2,1:T(8,128)S(1)}, u32[]{:S(2)}, u32[]{:S(2)}) collective-permute-start(f32[32,10,1,128]{3,0,2,1:T(8,128)S(1)} %get-tuple-element.15), channel_id=1, source_target_pairs={{0,4},{1,5},{2,6},{3,7},{8,12},{9,13},{10,14},{11,15},{16,20},{17,... | collective-permute-start | bytes 491528 | tf_op jit(solution)/shard_map/ppermute | solution.py:14
  99.8 3.3 %collective-permute-start.2 = (f32[32,10,1,128]{3,0,2,1:T(8,128)S(1)}, f32[32,10,1,128]{3,0,2,1:T(8,128)S(1)}, u32[]{:S(2)}, u32[]{:S(2)}) collective-permute-start(f32[32,10,1,128]{3,0,2,1:T(8,128)S(1)} %get-tuple-element.16), channel_id=1, source_target_pairs={{4,0},{5,1},{6,2},{7,3},{12,8},{13,9},{14,10},{15,11},{20,16},{21,... | collective-permute-start | bytes 491528 | tf_op jit(solution)/shard_map/ppermute | solution.py:17
  108.1 7.9 %collective-permute-start.4 = (f32[32,10,10,1]{0,3,2,1:T(1,128)S(1)}, f32[32,10,10,1]{0,3,2,1:T(1,128)S(1)}, u32[]{:S(2)}, u32[]{:S(2)}) collective-permute-start(f32[32,10,10,1]{0,3,2,1:T(1,128)S(1)} %copy.13), channel_id=1, source_target_pairs={{1,0},{2,1},{3,2},{5,4},{6,5},{7,6},{9,8},{10,9},{11,10},{13,12},{... | collective-permute-start | bytes 38408 | tf_op jit(solution)/shard_map/ppermute | solution.py:17
  111.5 6.4 %collective-permute-start.5 = (f32[32,10,10,1]{0,3,2,1:T(1,128)S(1)}, f32[32,10,10,1]{0,3,2,1:T(1,128)S(1)}, u32[]{:S(2)}, u32[]{:S(2)}) collective-permute-start(f32[32,10,10,1]{0,3,2,1:T(1,128)S(1)} %copy.15), channel_id=1, source_target_pairs={{0,1},{1,2},{2,3},{4,5},{5,6},{6,7},{8,9},{9,10},{10,11},{12,13},{... | collective-permute-start | bytes 38408 | tf_op jit(solution)/shard_map/ppermute | solution.py:14
  122.7 6.2 %collective-permute-start.7 = (f32[32,1,8,128]{3,0,2,1:T(8,128)S(1)}, f32[32,1,8,128]{3,0,2,1:T(8,128)S(1)}, u32[]{:S(2)}, u32[]{:S(2)}) collective-permute-start(f32[32,1,8,128]{3,0,2,1:T(8,128)S(1)} %get-tuple-element.19), channel_id=1, source_target_pairs={{0,8},{8,16},{16,24},{1,9},{9,17},{17,25},{2,10},{10,18},{18,26},{... | collective-permute-start | bytes 393224 | tf_op jit(solution)/shard_map/ppermute | solution.py:14
  126.3 6.9 %collective-permute-start.6 = (f32[32,1,8,128]{3,0,2,1:T(8,128)S(1)}, f32[32,1,8,128]{3,0,2,1:T(8,128)S(1)}, u32[]{:S(2)}, u32[]{:S(2)}) collective-permute-start(f32[32,1,8,128]{3,0,2,1:T(8,128)S(1)} %get-tuple-element.20), channel_id=1, source_target_pairs={{8,0},{16,8},{24,16},{9,1},{17,9},{25,17},{10,2},{18,10},{26,18},{... | collective-permute-start | bytes 393224 | tf_op jit(solution)/shard_map/ppermute | solution.py:17
  133.2 2.6 %collective-permute-start.9 = (f32[32,10,1,128]{3,0,2,1:T(8,128)S(1)}, f32[32,10,1,128]{3,0,2,1:T(8,128)S(1)}, u32[]{:S(2)}, u32[]{:S(2)}) collective-permute-start(f32[32,10,1,128]{3,0,2,1:T(8,128)S(1)} %get-tuple-element.13), channel_id=1, source_target_pairs={{0,4},{1,5},{2,6},{3,7},{8,12},{9,13},{10,14},{11,15},{16,20},{17,... | collective-permute-start | bytes 491528 | tf_op jit(solution)/shard_map/ppermute | solution.py:14
  134.5 3.3 %collective-permute-start.8 = (f32[32,10,1,128]{3,0,2,1:T(8,128)S(1)}, f32[32,10,1,128]{3,0,2,1:T(8,128)S(1)}, u32[]{:S(2)}, u32[]{:S(2)}) collective-permute-start(f32[32,10,1,128]{3,0,2,1:T(8,128)S(1)} %get-tuple-element.14), channel_id=1, source_target_pairs={{4,0},{5,1},{6,2},{7,3},{12,8},{13,9},{14,10},{15,11},{20,16},{21,... | collective-permute-start | bytes 491528 | tf_op jit(solution)/shard_map/ppermute | solution.py:17
  143.0 8.2 %collective-permute-start.10 = (f32[32,10,10,1]{0,3,2,1:T(1,128)S(1)}, f32[32,10,10,1]{0,3,2,1:T(1,128)S(1)}, u32[]{:S(2)}, u32[]{:S(2)}) collective-permute-start(f32[32,10,10,1]{0,3,2,1:T(1,128)S(1)} %copy.17), channel_id=1, source_target_pairs={{1,0},{2,1},{3,2},{5,4},{6,5},{7,6},{9,8},{10,9},{11,10},{13,12},{... | collective-permute-start | bytes 38408 | tf_op jit(solution)/shard_map/ppermute | solution.py:17
  146.4 6.6 %collective-permute-start.11 = (f32[32,10,10,1]{0,3,2,1:T(1,128)S(1)}, f32[32,10,10,1]{0,3,2,1:T(1,128)S(1)}, u32[]{:S(2)}, u32[]{:S(2)}) collective-permute-start(f32[32,10,10,1]{0,3,2,1:T(1,128)S(1)} %copy.19), channel_id=1, source_target_pairs={{0,1},{1,2},{2,3},{4,5},{5,6},{6,7},{8,9},{9,10},{10,11},{12,13},{... | collective-permute-start | bytes 38408 | tf_op jit(solution)/shard_map/ppermute | solution.py:14
  157.8 5.6 %collective-permute-start.13 = (f32[32,1,8,128]{3,0,2,1:T(8,128)S(1)}, f32[32,1,8,128]{3,0,2,1:T(8,128)S(1)}, u32[]{:S(2)}, u32[]{:S(2)}) collective-permute-start(f32[32,1,8,128]{3,0,2,1:T(8,128)S(1)} %get-tuple-element.17), channel_id=1, source_target_pairs={{0,8},{8,16},{16,24},{1,9},{9,17},{17,25},{2,10},{10,18},{18,26},{... | collective-permute-start | bytes 393224 | tf_op jit(solution)/shard_map/ppermute | solution.py:14
  160.6 6.9 %collective-permute-start.12 = (f32[32,1,8,128]{3,0,2,1:T(8,128)S(1)}, f32[32,1,8,128]{3,0,2,1:T(8,128)S(1)}, u32[]{:S(2)}, u32[]{:S(2)}) collective-permute-start(f32[32,1,8,128]{3,0,2,1:T(8,128)S(1)} %get-tuple-element.18), channel_id=1, source_target_pairs={{8,0},{16,8},{24,16},{9,1},{17,9},{25,17},{10,2},{18,10},{26,18},{... | collective-permute-start | bytes 393224 | tf_op jit(solution)/shard_map/ppermute | solution.py:17
  167.5 2.6 %collective-permute-start.15 = (f32[32,10,1,128]{3,0,2,1:T(8,128)S(1)}, f32[32,10,1,128]{3,0,2,1:T(8,128)S(1)}, u32[]{:S(2)}, u32[]{:S(2)}) collective-permute-start(f32[32,10,1,128]{3,0,2,1:T(8,128)S(1)} %get-tuple-element.11), channel_id=1, source_target_pairs={{0,4},{1,5},{2,6},{3,7},{8,12},{9,13},{10,14},{11,15},{16,20},{17,... | collective-permute-start | bytes 491528 | tf_op jit(solution)/shard_map/ppermute | solution.py:14
  168.9 3.3 %collective-permute-start.14 = (f32[32,10,1,128]{3,0,2,1:T(8,128)S(1)}, f32[32,10,1,128]{3,0,2,1:T(8,128)S(1)}, u32[]{:S(2)}, u32[]{:S(2)}) collective-permute-start(f32[32,10,1,128]{3,0,2,1:T(8,128)S(1)} %get-tuple-element.12), channel_id=1, source_target_pairs={{4,0},{5,1},{6,2},{7,3},{12,8},{13,9},{14,10},{15,11},{20,16},{21,... | collective-permute-start | bytes 491528 | tf_op jit(solution)/shard_map/ppermute | solution.py:17
  177.1 9.7 %collective-permute-start.16 = (f32[32,10,10,1]{0,3,2,1:T(1,128)S(1)}, f32[32,10,10,1]{0,3,2,1:T(1,128)S(1)}, u32[]{:S(2)}, u32[]{:S(2)}) collective-permute-start(f32[32,10,10,1]{0,3,2,1:T(1,128)S(1)} %copy.21), channel_id=1, source_target_pairs={{1,0},{2,1},{3,2},{5,4},{6,5},{7,6},{9,8},{10,9},{11,10},{13,12},{... | collective-permute-start | bytes 38408 | tf_op jit(solution)/shard_map/ppermute | solution.py:17
  181.3 10.0 %copy-start.2 = (f32[32,8,8,128]{3,2,1,0:T(8,128)S(1)}, f32[32,8,8,128]{3,2,1,0:T(8,128)}, u32[]{:S(2)}) copy-start(f32[32,8,8,128]{3,2,1,0:T(8,128)} %param.8) | copy-start | bytes 3145732
  181.3 7.4 %collective-permute-start.17 = (f32[32,10,10,1]{0,3,2,1:T(1,128)}, f32[32,10,10,1]{0,3,2,1:T(1,128)}, u32[]{:S(2)}, u32[]{:S(2)}) collective-permute-start(f32[32,10,10,1]{0,3,2,1:T(1,128)} %copy.23), channel_id=1, source_target_pairs={{0,1},{1,2},{2,3},{4,5},{5,6},{6,7},{8,9},{9,10},{10,11},{12,13},{... | collective-permute-start | bytes 38408 | tf_op jit(solution)/shard_map/ppermute | solution.py:14
  (6 other events, 8.3 us)
Sparse Core Ops, SparseCore 0:
  14.2 64.3 all-gather.2
